TPU v7x, 32 devices: a whole 2x2x4 slice. The times are simulated.
32 devices in a mesh: ctx: 16 (over z, x, core), fsdp: 2 (over y).
Axes of the slice: x: 2, y: 2, z: 4, core: 2. Of those that a mesh axis runs over, the one named last changes fastest.
Arguments:
- layer_input: bfloat16 [2048, 4096], P('ctx'), may hold values from -8 to 8
- gain: float32 [4096], replicated, may hold values from 0.5 to 1.5
- codes: int32 [4096, 384], P('fsdp'), may hold values from -2147483648 to 2147483646
- column_scale_quantized: int32 [64, 3072], P('fsdp'), may hold values from 0 to 255
- block_second_scale: float32 [64], replicated, may hold values from 0.03 to 0.12
- query_down_map: bfloat16 [4096, 16], replicated, may hold values from -0.09375 to 0.09375
- query_up_map: bfloat16 [16, 2048], P(None, 'fsdp'), may hold values from -0.29882812 to 0.29882812
- token_document: int32 [2048], P('ctx'), may hold values from 0 to 3, as said below
- output_cotangent: bfloat16 [2048, 2048], P('ctx', 'fsdp'), may hold values from -0.059814453 to 0.059814453
Outputs:
- attn: bfloat16 [2048, 2048], P('ctx', 'fsdp')
- grad_a: float32 [4096, 16], replicated
- up_map_gradient: float32 [16, 2048], P(None, 'fsdp')
Inputs may be any that keep to these rules, and one draw needn't show every extreme that they name: token_document never falls along the sequence; each document has 1 to 1536 tokens and one has exactly 1536.
All inputs are finite; a program needn't handle non-finite values.
Results may differ from a plain program's by a relative error of at most 0.028.
Values may be sent and summed in bfloat16 or wider, within the bound.
A program may use at most 192 MiB of HBM per device.

v0:
```python
import math

import jax
import jax.numpy as jnp
from jax import lax
from jax.sharding import PartitionSpec as P

QUERY_HEADS = 16
KEY_VALUE_HEADS = 4
HEAD_SIZE = 128


NF4_LEVELS = [
    -1.0,
    -0.6961928009986877,
    -0.5250730514526367,
    -0.39491748809814453,
    -0.28444138169288635,
    -0.18477343022823334,
    -0.09105003625154495,
    0.0,
    0.07958029955625534,
    0.16093020141124725,
    0.24611230194568634,
    0.33791524171829224,
    0.44070982933044434,
    0.5626170039176941,
    0.7229568362236023,
    1.0,
]
ADAPTER_SCALE = 2.0
ROPE_BASE = 500000.0


def dequantize(packed, column_scale_quantized, block_second_scale):
    row_count = packed.shape[0]
    pieces = [jnp.bitwise_and(jnp.right_shift(packed, 4 * nibble), 15) for nibble in range(8)]
    unpacked = jnp.stack(pieces, axis=-1).reshape(row_count, packed.shape[1] * 8)
    levels = jnp.zeros(unpacked.shape, jnp.float32)
    for slot_code, level_value in enumerate(NF4_LEVELS):
        levels = levels + jnp.where(
            unpacked == slot_code, jnp.float32(level_value), jnp.float32(0.0)
        )
    absmax = (
        (column_scale_quantized.astype(jnp.float32) + 1.0) / 256.0 * block_second_scale[:, None]
    )
    scaled = levels.reshape(row_count // 64, 64, -1) * absmax[:, None, :]
    return scaled.reshape(row_count, -1).astype(jnp.bfloat16)


def rope_angles(positions):
    freqs = jnp.exp(
        jnp.arange(HEAD_SIZE // 2, dtype=jnp.float32) * (-2.0 * math.log(ROPE_BASE) / HEAD_SIZE)
    )
    angle = positions.astype(jnp.float32)[:, None] * freqs[None, :]
    cosine = jnp.concatenate([jnp.cos(angle), jnp.cos(angle)], axis=-1)
    sine = jnp.concatenate([jnp.sin(angle), jnp.sin(angle)], axis=-1)
    return (cosine, sine)


def apply_rotation(field, rotary_phases):
    cosine, sine = rotary_phases
    half = HEAD_SIZE // 2
    turned = jnp.concatenate([-field[..., half:], field[..., :half]], axis=-1)
    return field * cosine[:, None, :] + turned * sine[:, None, :]


def rotate_back(grads, rotary_phases):
    cosine, sine = rotary_phases
    half = HEAD_SIZE // 2
    scaled = grads * sine[:, None, :]
    turned = jnp.concatenate([-scaled[..., half:], scaled[..., :half]], axis=-1)
    return grads * cosine[:, None, :] - turned


def rms_norm(layer_input, gain):
    wide = layer_input.astype(jnp.float32)
    inverse = lax.rsqrt(jnp.mean(wide * wide, axis=-1, keepdims=True) + 1e-05)
    return (wide * inverse * gain[None, :]).astype(jnp.bfloat16)


def fresh_state(head_count, head_grouped, row_count):
    small = jnp.zeros((head_count, head_grouped, row_count), jnp.float32)
    large = jnp.zeros((head_count, head_grouped, row_count, HEAD_SIZE), jnp.float32)
    return (small - 1e30, small, small, large, large, large)


def on_device(
    layer_input,
    gain,
    codes,
    column_scale_quantized,
    block_second_scale,
    query_down_map,
    query_up_map,
    token_document,
    output_cotangent,
):
    row_count = layer_input.shape[0]
    group_total = lax.axis_size("fsdp")
    member = lax.axis_index("fsdp")
    my_place = lax.axis_index("ctx")
    query_width = query_up_map.shape[1]
    heads_here = query_width // HEAD_SIZE
    key_value_heads = KEY_VALUE_HEADS // group_total
    kv_width = key_value_heads * HEAD_SIZE
    group_columns = column_scale_quantized.shape[1] // group_total
    head_grouped = QUERY_HEADS // KEY_VALUE_HEADS
    soft_scale = 1.0 / math.sqrt(HEAD_SIZE)
    all_codes, all_scales = (
        lax.all_gather(codes, "fsdp", axis=0, tiled=True),
        lax.all_gather(column_scale_quantized, "fsdp", axis=0, tiled=True),
    )
    my_codes = lax.dynamic_slice_in_dim(
        all_codes, member * (group_columns // 8), group_columns // 8, 1
    )
    my_scales = lax.dynamic_slice_in_dim(all_scales, member * group_columns, group_columns, 1)
    weight = dequantize(my_codes, my_scales, block_second_scale)
    input_normalized = rms_norm(layer_input, gain)
    projection_output = jnp.dot(input_normalized, weight, preferred_element_type=jnp.float32)
    rank_reduced = jnp.dot(
        input_normalized, query_down_map, preferred_element_type=jnp.float32
    ).astype(jnp.bfloat16)
    query_complete = projection_output[:, :query_width] + ADAPTER_SCALE * jnp.dot(
        rank_reduced, query_up_map, preferred_element_type=jnp.float32
    )
    positions = my_place * row_count + jnp.arange(row_count, dtype=jnp.int32)
    last_position = my_place * row_count + row_count - 1
    rotary_phases = rope_angles(positions)
    query_rows = apply_rotation(
        query_complete.reshape(row_count, heads_here, HEAD_SIZE), rotary_phases
    ).astype(jnp.bfloat16)
    key_rows = apply_rotation(
        projection_output[:, query_width : query_width + kv_width].reshape(
            row_count, key_value_heads, HEAD_SIZE
        ),
        rotary_phases,
    ).astype(jnp.bfloat16)
    value_rows = (
        projection_output[:, query_width + kv_width :]
        .reshape(row_count, key_value_heads, HEAD_SIZE)
        .astype(jnp.bfloat16)
    )
    query_grouped = query_rows.reshape(row_count, key_value_heads, head_grouped, HEAD_SIZE)
    grouped_gradient = output_cotangent.reshape(row_count, key_value_heads, head_grouped, HEAD_SIZE)
    all_ids = lax.all_gather(token_document, "ctx", axis=0, tiled=True)

    def update(state, query_part, grad_part, key_part, value_part, key_start):
        key_count = key_part.shape[0]
        key_pos = key_start + jnp.arange(key_count, dtype=jnp.int32)
        key_ids = lax.dynamic_slice_in_dim(all_ids, key_start, key_count, 0)
        allowed = (token_document[:, None] == key_ids[None, :]) & (
            key_pos[None, :] <= positions[:, None]
        )

        def work(carry):
            run_max, run_sum, run_dot, run_out, run_grad, run_key = carry
            scores = (
                jnp.einsum(
                    "qhgd,khd->hgqk", query_part, key_part, preferred_element_type=jnp.float32
                )
                * soft_scale
            )
            masked = jnp.where(allowed, scores, -1e30)
            new_max = jnp.maximum(run_max, jnp.max(masked, axis=-1))
            expo = jnp.where(allowed, jnp.exp(masked - new_max[..., None]), 0.0)
            decay = jnp.exp(run_max - new_max)
            grad_dots = jnp.einsum(
                "qhgd,khd->hgqk", grad_part, value_part, preferred_element_type=jnp.float32
            )
            weighted = expo * grad_dots
            expo_low = expo.astype(jnp.bfloat16)
            run_sum = decay * run_sum + jnp.sum(expo, axis=-1)
            run_dot = decay * run_dot + jnp.sum(weighted, axis=-1)
            run_out = decay[..., None] * run_out + jnp.einsum(
                "hgqk,khd->hgqd", expo_low, value_part, preferred_element_type=jnp.float32
            )
            run_key = decay[..., None] * run_key + jnp.einsum(
                "hgqk,khd->hgqd", expo_low, key_part, preferred_element_type=jnp.float32
            )
            run_grad = decay[..., None] * run_grad + jnp.einsum(
                "hgqk,khd->hgqd",
                weighted.astype(jnp.bfloat16),
                key_part,
                preferred_element_type=jnp.float32,
            )
            return (new_max, run_sum, run_dot, run_out, run_grad, run_key)

        def unchanged(carry):
            return carry

        active = key_start <= last_position
        return lax.cond(active, work, unchanged, state)

    start_state = fresh_state(key_value_heads, head_grouped, row_count)
    key_piece = lax.all_gather(key_rows, "ctx", axis=0, tiled=True)
    value_piece = lax.all_gather(value_rows, "ctx", axis=0, tiled=True)
    piece_len = key_piece.shape[0]
    key_block = math.gcd(piece_len, max(row_count, 512))
    block_count = piece_len // key_block

    def inner_block(number, carried):
        offset = number * key_block
        key_part = lax.dynamic_slice_in_dim(key_piece, offset, key_block, 0)
        value_part = lax.dynamic_slice_in_dim(value_piece, offset, key_block, 0)
        return update(carried, query_grouped, grouped_gradient, key_part, value_part, offset)

    state = lax.fori_loop(0, block_count, inner_block, start_state)
    run_max, run_sum, run_dot, run_out, run_grad, run_key = state
    output = run_out / run_sum[..., None]
    attn = jnp.transpose(output, (2, 0, 1, 3)).reshape(row_count, query_width).astype(jnp.bfloat16)
    mean_dot = run_dot / run_sum
    grad_query = soft_scale * (run_grad - mean_dot[..., None] * run_key) / run_sum[..., None]
    grad_query = jnp.transpose(grad_query, (2, 0, 1, 3)).reshape(row_count, heads_here, HEAD_SIZE)
    linear_gradient = (
        rotate_back(grad_query, rotary_phases).reshape(row_count, query_width).astype(jnp.bfloat16)
    )
    local_up_map = ADAPTER_SCALE * jnp.dot(
        rank_reduced.T, linear_gradient, preferred_element_type=jnp.float32
    )
    middle_gradient = (
        ADAPTER_SCALE * jnp.dot(linear_gradient, query_up_map.T, preferred_element_type=jnp.float32)
    ).astype(jnp.bfloat16)
    local_a = jnp.dot(input_normalized.T, middle_gradient, preferred_element_type=jnp.float32)
    up_map_gradient = lax.psum(local_up_map, "ctx")
    grad_a = lax.psum(local_a, ("ctx", "fsdp"))
    return (attn, grad_a, up_map_gradient)


def solution(mesh):
    return jax.shard_map(
        on_device,
        mesh=mesh,
        in_specs=(
            P("ctx", None),
            P(),
            P("fsdp", None),
            P("fsdp", None),
            P(),
            P(),
            P(None, "fsdp"),
            P("ctx"),
            P("ctx", "fsdp"),
        ),
        out_specs=(P("ctx", "fsdp"), P(), P(None, "fsdp")),
        check_vma=False,
    )
```

profile of v0, /device:TPU:0, one launch (start us, length us, event | category | flops | bytes accessed | tf_op | source)
XLA Modules:
  0.0 597.2 jit_solution(3610667669623867392)
XLA Ops:
  7.2 3.6 copy.113
  10.9 0.9 copy-done.7
  11.9 12.8 %all_gather.17 = s32[64,3072]{1,0:T(8,128)S(1)} all-gather(s32[32,3072]{1,0:T(8,128)S(1)} %copy-done.7), channel_id=1, replica_groups=mesh['ctx'=16,'fsdp'=2] {'fsdp'}, dimensions={0}, use_global_device_ids=true | all-gather | bytes 1179648 | tf_op jit(solution)/shard_map/all_gather | solution.py:112
  24.7 11.9 %mul.238 = f32[64,64,1536]{2,1,0:T(8,128)} broadcast(f32[64,1536]{1,0:T(8,128)S(1)} %add_multiply_fusion), dimensions={0,2} | broadcast | bytes 25559040 | tf_op jit(solution)/shard_map/mul | solution.py:47
  36.6 24.8 %copy.121 = f32[4096,1536]{0,1:T(8,128)} copy(f32[4096,1536]{1,0:T(8,128)} %bitcast.119) | data formatting | bytes 50331648 | tf_op jit(solution)/shard_map/mul | solution.py:47
  62.2 31.9 %all-gather.5.cloned.1.call-done = s32[4096,384]{0,1:T(8,128)} async-done(((s32[2048,384]{0,1:T(8,128)}), s32[4096,384]{0,1:T(8,128)}) %all-gather.5.cloned.1.call-update) | async-done | bytes 6291472 | tf_op jit(solution)/shard_map/all_gather | solution.py:111
  94.1 6.2 %shift-right-arithmetic_and_fusion = (s32[4096,192]{0,1:T(8,128)}, s32[4096,192,1]{0,1,2:T(8,128)}, s32[4096,192,1]{0,1,2:T(8,128)S(1)}, s32[4096,192,1]{0,1,2:T...) fusion(s32[4096,384]{0,1:T(8,128)} %all-gather.5.cloned.1.call-, ...), kind=kLoop, calls=%fused_computation.36 | loop fusion | flops 12582912 | bytes 28311556 | tf_op jit(solution)/shard_map/and | solution.py:37
  100.3 6.8 %copy.114 = s32[4096,192,1]{0,2,1:T(1,128)} copy(s32[4096,192,1]{0,1,2:T(8,128)} %get-tuple-element.617) | data formatting | bytes 6291456 | tf_op jit(solution)/shard_map/stack | solution.py:38
  107.1 6.8 %copy.115 = s32[4096,192,1]{0,2,1:T(1,128)} copy(s32[4096,192,1]{0,1,2:T(8,128)} %get-tuple-element.611) | data formatting | bytes 6291456 | tf_op jit(solution)/shard_map/stack | solution.py:38
  113.9 4.9 copy.116
  118.8 5.0 copy.117
  123.8 4.9 copy.118
  128.6 4.9 copy.119
  133.6 5.0 copy.120
  138.5 7.4 %stack.34 = s32[4096,192,1]{0,2,1:T(1,128)} reshape(s32[4096,192]{0,1:T(8,128)} %get-tuple-element.610) | data formatting | bytes 6291456 | tf_op jit(solution)/shard_map/stack | solution.py:38
  145.9 66.3 %stack.35 = s32[4096,192,8]{0,2,1:T(8,128)} concatenate(s32[4096,192,1]{0,2,1:T(1,128)} %copy.114, s32[4096,192,1]{0,2,1:T(1,128)} %copy.115, s32[4096,192,1]{0,2,1:T(1,128)} %copy.116, s32[4096,192,1]{0,2,1:T(1,128)} %copy.117, s32[4096,192,1]{0,2,1:T(1,128)} %copy.118, s32[4096,192,1]{0,2,1:T(1,128)} %copy.119, s32[4096,192,1]{0,2,1:T(1,128)} %copy.120, s32[4096,192,1]{0,2,1:T(1,128)} %stack.34), dimensions={2} | concatenate | bytes 50331648 | tf_op jit(solution)/shard_map/stack | solution.py:38
  212.3 42.3 %fusion.25 = f32[128,1536]{1,0:T(8,128)S(1)} fusion(f32[4096,1536]{0,1:T(8,128)} %copy.121, s32[4096,192,8]{0,2,1:T(8,128)} %stack.35, bf16[128,4096]{1,0:T(8,128)(2,1)S(1)} %copy-done.2, f32[4096]{0:T(1024)S(1)} %copy-done.12, f32[128]{0:T(128)S(1)} %add_rsqrt_fusion), kind=kOutput, calls=%fused_computation.35 | convolution fusion | flops 1902116864 | bytes 52183552 | tf_op jit(solution)/shard_map/dot_general | solution.py:120
  256.6 21.3 %all-gather = s32[16,1,128]{2,1,0:T(1,128)S(1)} all-gather(s32[1,1,128]{2,1,0:T(1,128)S(1)} %bitcast.138), channel_id=1, replica_groups=mesh['ctx'=16,'fsdp'=2] {'ctx'}, dimensions={0}, use_global_device_ids=true | all-gather | bytes 8704 | tf_op jit(solution)/shard_map/all_gather | solution.py:146
  279.9 13.7 %all-gather.7.cloned.1.call-done = bf16[2048,2,128]{2,0,1:T(8,128)(2,1)} async-done(((bf16[128,2,128]{2,0,1:T(8,128)(2,1)}), bf16[2048,2,128]{2,0,1:T(8,128)(2,1)}) %all-gather.7.cloned.1.call-update) | async-done | bytes 1048592 | tf_op jit(solution)/shard_map/all_gather | solution.py:196
  293.5 39.6 %all-gather.9.cloned.1.call-done = bf16[2048,2,128]{2,0,1:T(8,128)(2,1)} async-done(((bf16[128,2,128]{2,0,1:T(8,128)(2,1)}), bf16[2048,2,128]{2,0,1:T(8,128)(2,1)}) %all-gather.9.cloned.1.call-update) | async-done | bytes 1048592 | tf_op jit(solution)/shard_map/all_gather | solution.py:197
  333.3 8.3 %while.24 = (s32[]{:T(128)}, f32[2,4,128]{2,1,0:T(4,128)S(1)}, f32[2,4,128]{2,1,0:T(4,128)S(1)}, f32[2,4,128]{2,1,0:T(4,128)S(1)}, f32[2,4,128,128]{3,2,1,0:T(8,...) while((s32[]{:T(128)}, f32[2,4,128]{2,1,0:T(4,128)S(1)}, ...), condition=%wide.region_7.8_spmd.clone, body=%wide.region_1.7_spmd.clone.sunk | while | flops 685182592 | bytes 22270972 | solution.py:208
  333.6 7.8 %conditional.3 = ((f32[2,4,128]{2,1,0:T(4,128)S(1)}, f32[2,4,128]{2,1,0:T(4,128)S(1)}, f32[2,4,128]{2,1,0:T(4,128)S(1)}, f32[2,4,128,128]{3,2,1,0:T(8,128)S(1)},...) conditional(s32[]{:T(128)} %convert_element_type.124, (f32[2,4,128]{2,1,0:T(4,128)S(1)}, ...), branch_computations={%region_2.2_spmd, %region_3.6_spmd} | conditional | flops 685182592 | bytes 22268054 | solution.py:193
  333.9 1.4 fusion.2
  335.4 1.9 fusion.76
  337.3 0.9 convolution_add_fusion
  339.0 1.9 convolution_add_fusion.2
  342.5 1.0 bitcast_multiply_fusion.2
  344.6 1.2 fusion.32
  346.6 106.7 %all-reduce.5.cloned.1.call-done = f32[16,1024]{1,0:T(8,128)} async-done(((f32[16,1024]{1,0:T(8,128)}), f32[16,1024]{1,0:T(8,128)}) %all-reduce.5.cloned.1.call-update) | async-done | bytes 65552 | tf_op jit(solution)/shard_map/psum | solution.py:225
  453.3 134.0 %all-reduce.3.cloned.1.call-done = f32[4096,16]{0,1:T(8,128)} async-done(((f32[4096,16]{0,1:T(8,128)}), f32[4096,16]{0,1:T(8,128)}) %all-reduce.3.cloned.1.call-update) | async-done | bytes 262160 | tf_op jit(solution)/shard_map/psum | solution.py:226
  587.3 1.7 copy.191
  588.9 1.5 copy.192
  (100 shorter events, 9.2 us)
Async XLA Ops:
  7.2 270.8 %copy-start = (bf16[4096,16]{0,1:T(8,128)(2,1)S(1)}, bf16[4096,16]{0,1:T(8,128)(2,1)}, u32[]{:S(2)}) copy-start(bf16[4096,16]{0,1:T(8,128)(2,1)} %param.18) | copy-start | bytes 393220
  7.2 86.9 %all-gather.5.cloned.1.call-start = ((), (), s32[]{:S(2)}) async-start(), calls=%async_computation | async-start | bytes 9437184 | tf_op jit(solution)/shard_map/all_gather | solution.py:111
  10.9 1.0 copy-start.7
  10.9 13.8 %copy-start.14 = (f32[64]{0:T(128)S(1)}, f32[64]{0:T(128)}, u32[]{:S(2)}) copy-start(f32[64]{0:T(128)} %param.17) | copy-start | bytes 772
  10.9 282.6 %all-gather.7.cloned.1.call-start = ((), (), s32[]{:S(2)}) async-start(), calls=%async_computation.1 | async-start | bytes 1114112 | tf_op jit(solution)/shard_map/all_gather | solution.py:196
  36.6 25.3 %copy-start.2 = (bf16[128,4096]{1,0:T(8,128)(2,1)S(1)}, bf16[128,4096]{1,0:T(8,128)(2,1)}, u32[]{:S(2)}) copy-start(bf16[128,4096]{1,0:T(8,128)(2,1)} %param.13) | copy-start | bytes 3145732
  61.7 38.6 %copy-start.4 = (f32[128,128]{0,1:T(8,128)}, f32[128,128]{0,1:T(8,128)S(1)}, u32[]{:S(2)}) copy-start(f32[128,128]{0,1:T(8,128)S(1)} %get-tuple-element.629) | copy-start | bytes 196612
  61.7 38.6 %copy-start.5 = (f32[128,128]{0,1:T(8,128)}, f32[128,128]{0,1:T(8,128)S(1)}, u32[]{:S(2)}) copy-start(f32[128,128]{0,1:T(8,128)S(1)} %get-tuple-element.628) | copy-start | bytes 196612
  145.9 66.3 %copy-start.12 = (f32[4096]{0:T(1024)S(1)}, f32[4096]{0:T(1024)}, u32[]{:S(2)}) copy-start(f32[4096]{0:T(1024)} %param.14) | copy-start | bytes 49156
  212.2 44.0 %copy-start.8 = (bf16[128,1024]{1,0:T(8,128)(2,1)S(1)}, bf16[128,1024]{1,0:T(8,128)(2,1)}, u32[]{:S(2)}) copy-start(bf16[128,1024]{1,0:T(8,128)(2,1)} %param.21) | copy-start | bytes 786436
  212.3 44.3 %copy-start.11 = (s32[128]{0:T(128)S(1)}, s32[128]{0:T(128)}, u32[]{:S(2)}) copy-start(s32[128]{0:T(128)} %param.20) | copy-start | bytes 1540
  254.5 23.9 %copy-start.9 = (bf16[16,1024]{1,0:T(8,128)(2,1)S(1)}, bf16[16,1024]{1,0:T(8,128)(2,1)}, u32[]{:S(2)}) copy-start(bf16[16,1024]{1,0:T(8,128)(2,1)} %param.19) | copy-start | bytes 98308
  255.4 77.7 %all-gather.9.cloned.1.call-start = ((), (), s32[]{:S(2)}) async-start(), calls=%async_computation.2 | async-start | bytes 1114112 | tf_op jit(solution)/shard_map/all_gather | solution.py:197
  256.2 197.1 %all-reduce.5.cloned.1.call-start = ((), (), s32[]{:S(2)}) async-start(), calls=%async_computation.4 | async-start | bytes 131072 | tf_op jit(solution)/shard_map/psum | solution.py:225
  335.4 1.9 copy-start.1
  342.3 1.3 copy-start.6
  342.3 2.2 copy-start.3
  342.4 2.1 copy-start.10
  342.5 2.1 copy-start.13
  344.5 242.8 %all-reduce.3.cloned.1.call-start = ((), (), s32[]{:S(2)}) async-start(), calls=%async_computation.3 | async-start | bytes 524288 | tf_op jit(solution)/shard_map/psum | solution.py:226
Sparse Core Ops, SparseCore 0:
  11.0 83.0 all-gather.4
  255.5 37.9 all-gather.6
  296.3 36.8 all-gather.8
  344.6 108.6 all-reduce.4
  459.2 128.0 all-reduce.2
where the time goes:
time: 609 us; the launch traced here: 597 us
  waiting for transfers between devices  326 us (54%)
  local copies, waits for them, and re-layouts  160 us (26%)
  matrix products  51.8 us (9%)
  blocking collectives  34.1 us (6%)
  between operations  14.5 us (2%)
  other arithmetic  9.96 us (2%)
    psum x1, waiting for transfers between devices, on_device(): grad_a = lax.psum(local_a, ('ctx', 'fsdp'))  134 us
    another operation x9, local copies, waits for them, and re-layouts, dequantize(): jnp.stack(pieces, axis=-1).reshape(row_count, packed.shape[1] * 8)  112 us
    psum x1, waiting for transfers between devices, on_device(): up_map_gradient = lax.psum(local_up_map, 'ctx')  107 us
    dot_general x1, matrix products, on_device(): jnp.dot(input_normalized, weight, preferred_element_type=jnp.float32)  42.3 us
    all_gather x1, waiting for transfers between devices, on_device(): value_piece = lax.all_gather(value_rows, 'ctx', axis=0, tiled=True)  39.6 us
    mul x2, local copies, waits for them, and re-layouts, dequantize(): scaled = levels.reshape(row_count // 64, 64, -1) * absmax[:, None, :]  36.7 us
    all_gather x1, waiting for transfers between devices, on_device(): lax.all_gather(codes, 'fsdp', axis=0, tiled=True)  31.9 us
    all_gather x1, blocking collectives, on_device(): all_ids = lax.all_gather(token_document, 'ctx', axis=0, tiled=True)  21.3 us
  transfers between devices with their start and end apart: 5, of which 5 were waited for; matrix products, arithmetic and copies ran while one was open for 7% of the time, Pallas kernels for 0%

commit v1 on v0

v1 whole, which is shorter than its diff:
```python
import math
import functools

import jax
import jax.numpy as jnp
from jax import lax
from jax.experimental import pallas as pl
from jax.experimental.pallas import tpu as pltpu
from jax.sharding import PartitionSpec as P

QUERY_HEADS = 16
KEY_VALUE_HEADS = 4
HEAD_SIZE = 128
ADAPTER_SCALE = 2.0
ROPE_BASE = 500000.0
ID_ROWS = 16
MESH = pl.DeviceIdType.MESH
F32 = jnp.float32
BF16 = jnp.bfloat16

NF4_LEVELS = [
    -1.0,
    -0.6961928009986877,
    -0.5250730514526367,
    -0.39491748809814453,
    -0.28444138169288635,
    -0.18477343022823334,
    -0.09105003625154495,
    0.0,
    0.07958029955625534,
    0.16093020141124725,
    0.24611230194568634,
    0.33791524171829224,
    0.44070982933044434,
    0.5626170039176941,
    0.7229568362236023,
    1.0,
]


def take_lanes(values, index):
    return jnp.take_along_axis(values, index, axis=1, mode="promise_in_bounds")


def nt(a, b):
    return lax.dot_general(a, b, (((1,), (1,)), ((), ())), preferred_element_type=F32)


def tn(a, b):
    return lax.dot_general(a, b, (((0,), (0,)), ((), ())), preferred_element_type=F32)


def proj_kernel(
    x_ref, gain_ref, codes_ref, cs_ref, bss_ref, qdown_ref, qup_ref, ids_ref, cos_ref, sin_ref,
    q_ref, kv_ref, xn_ref, lr_ref,
    scl, vscl, acc, acct, own_kv, send_kv, recv_kv, send_q, recv_q, send_sem, recv_sem,
):
    member = lax.axis_index("fsdp")
    partner = 1 - member
    rows = x_ref.shape[0]
    width = x_ref.shape[1]
    depth = codes_ref.shape[0]
    blocks = cs_ref.shape[0]
    block_rows = depth // blocks
    half_lanes = 64

    barrier = pltpu.get_barrier_semaphore()
    pl.semaphore_signal(barrier, inc=1, device_id={"fsdp": partner}, device_id_type=MESH)
    pl.semaphore_wait(barrier, 1)

    lane = lax.broadcasted_iota(jnp.int32, (blocks, 128), 1)
    second = bss_ref[pl.ds(pl.multiple_of(member * blocks, 8), blocks), :]
    for tile in range(3):
        source = [
            (cs_ref[:, tile * 1024 + m * 128 : tile * 1024 + (m + 1) * 128].astype(F32) + 1.0)
            / 256.0
            * second
            for m in range(8)
        ]
        for n in range(8):
            index = 8 * (lane % 16) + n
            picked = take_lanes(source[0], index)
            for m in range(1, 8):
                picked = jnp.where(lane // 16 == m, take_lanes(source[m], index), picked)
            scl[tile * 8 + n] = picked

    for r in range(0, rows, 16):
        wide = x_ref[r : r + 16, :].astype(F32)
        inverse = lax.rsqrt(jnp.mean(wide * wide, axis=-1, keepdims=True) + 1e-05)
        xn_ref[r : r + 16, :] = (wide * inverse * gain_ref[...]).astype(BF16)
    lr_t = nt(qdown_ref[...], xn_ref[...]).astype(BF16)
    lr_ref[...] = lr_t

    level_lane = lax.broadcasted_iota(jnp.int32, (block_rows, 128), 1)
    table = jnp.zeros((block_rows, 128), F32)
    for code, level in enumerate(NF4_LEVELS):
        table = jnp.where(level_lane % 16 == code, F32(level), table)
    low_lanes = level_lane < half_lanes

    pr = lax.broadcasted_iota(jnp.int32, (128, 128), 0)
    pd = lax.broadcasted_iota(jnp.int32, (128, 128), 1)
    perm = (pd == 8 * (pr % 16) + pr // 16).astype(F32).astype(BF16)

    chunk = 512
    per_chunk = chunk // block_rows

    def phase(low_tile, high_tile):
        low_at = pl.multiple_of(low_tile * 128, 128)
        high_at = pl.multiple_of(high_tile * 128, 128)
        for n in range(8):
            vscl[n] = jnp.where(
                lane < half_lanes, scl[low_tile * 8 + n], scl[high_tile * 8 + n]
            )
        acc[...] = jnp.zeros_like(acc)

        def step(k, carry):
            lhs = xn_ref[:, pl.ds(pl.multiple_of(member * depth + k * chunk, 128), chunk)]
            words = []
            for b in range(per_chunk):
                at = pl.multiple_of(k * chunk + b * block_rows, block_rows)
                words.append(
                    jnp.where(
                        low_lanes,
                        codes_ref[pl.ds(at, block_rows), pl.ds(low_at, 128)],
                        codes_ref[pl.ds(at, block_rows), pl.ds(high_at, 128)],
                    )
                )
            for pair in range(4):
                planes = []
                for n in (2 * pair, 2 * pair + 1):
                    pieces = []
                    for b in range(per_chunk):
                        code = jnp.bitwise_and(jnp.right_shift(words[b], 4 * n), 15)
                        scale = vscl[n, pl.ds(k * per_chunk + b, 1), :]
                        pieces.append((take_lanes(table, code) * scale).astype(BF16))
                    planes.append(jnp.concatenate(pieces, axis=0))
                weight = jnp.concatenate(planes, axis=1)
                acc[:, pair * 256 : (pair + 1) * 256] += jnp.dot(
                    lhs, weight, preferred_element_type=F32
                )
            return carry

        lax.fori_loop(0, depth // chunk, step, 0)

    def turn(out):
        for n in range(8):
            out[n] = acc[:, n * 128 : (n + 1) * 128].T

    def exchange(src, dst, number):
        copy = pltpu.make_async_remote_copy(
            src_ref=src,
            dst_ref=dst,
            send_sem=send_sem.at[number],
            recv_sem=recv_sem.at[number],
            device_id={"fsdp": partner},
            device_id_type=MESH,
        )
        copy.start()
        return copy

    phase(1, 2)
    turn(acct)
    own_at = pl.multiple_of(member * 64, 64)
    other_at = pl.multiple_of(partner * 64, 64)
    send_kv[...] = acct[:, pl.ds(other_at, 64), :].astype(BF16)
    copy_kv = exchange(send_kv, recv_kv, 0)
    own_kv[...] = acct[:, pl.ds(own_at, 64), :]

    phase(2 * partner, partner)
    turn(acct)
    send_q[...] = acct[...].astype(BF16)
    copy_q = exchange(send_q, recv_q, 1)

    cosine = cos_ref[...].reshape(8, 8, rows)
    sine = sin_ref[...].reshape(8, 8, rows)

    def rotate(field):
        a, b = field[:, :8, :], field[:, 8:, :]
        return jnp.concatenate([a * cosine - b * sine, b * cosine + a * sine], axis=1)

    def natural(field):
        return tn(field.reshape(128, rows).astype(BF16), perm).astype(BF16)

    copy_kv.wait()
    for head in range(2):
        k_at, v_at = 16 * head, 32 + 16 * head
        key = own_kv[:, k_at : k_at + 16, :] + recv_kv[:, k_at : k_at + 16, :].astype(F32)
        kv_ref[:rows, head * 256 : head * 256 + 128] = natural(rotate(key))
        value = own_kv[:, v_at : v_at + 16, :] + recv_kv[:, v_at : v_at + 16, :].astype(F32)
        kv_ref[:rows, head * 256 + 128 : head * 256 + 256] = natural(value)
    ids = jnp.broadcast_to(ids_ref[...].astype(F32), (ID_ROWS, rows)).astype(BF16)
    kv_ref[rows:, :] = jnp.concatenate([ids] * 4, axis=1)

    phase(2 * member, member)
    turn(acct)
    copy_q.wait()
    for head in range(8):
        at = pl.multiple_of(16 * lax.rem(head + 4 * member, 8), 16)
        up_t = nt(perm, qup_ref[:, head * 128 : (head + 1) * 128]).astype(BF16)
        adapter = jnp.dot(up_t, lr_t, preferred_element_type=F32).reshape(8, 16, rows)
        query = acct[:, pl.ds(at, 16), :] + recv_q[:, pl.ds(at, 16), :].astype(F32)
        query = query + ADAPTER_SCALE * adapter
        q_ref[:, head * 128 : (head + 1) * 128] = natural(rotate(query))


def attn_kernel(
    first_ref, q_ref, do_ref, kv_ref, ids_ref, xn_ref, lr_ref, qup_ref, cos_ref, sin_ref,
    out_ref, up_ref, ga_ref,
    qs, dos, row_max, row_sum, row_dot, out_acc, grad_acc, lin,
):
    me = lax.axis_index("ctx")
    rows = q_ref.shape[0]
    soft_scale = 1.0 / math.sqrt(HEAD_SIZE)
    group = QUERY_HEADS // KEY_VALUE_HEADS
    many = group * rows
    my_ids = ids_ref[...]

    for head in range(8):
        at = head * rows
        qs[at : at + rows, :] = q_ref[:, head * 128 : (head + 1) * 128]
        dos[at : at + rows, :] = do_ref[:, head * 128 : (head + 1) * 128]

    def part(head, kv_part, allowed, first):
        span = pl.ds(head * many, many)
        key = kv_part[:, head * 256 : head * 256 + 128]
        value = kv_part[:, head * 256 + 128 : head * 256 + 256]
        both = kv_part[:, head * 256 : head * 256 + 256]
        scores = nt(qs[span, :], key) * soft_scale
        scores = jnp.where(jnp.concatenate([allowed] * group, axis=0), scores, -1e30)
        top = jnp.max(scores, axis=-1, keepdims=True)
        if not first:
            top = jnp.maximum(top, row_max[span, :])
        expo = jnp.exp(scores - top)
        weighted = expo * nt(dos[span, :], value)
        total = jnp.sum(expo, axis=-1, keepdims=True)
        dot_total = jnp.sum(weighted, axis=-1, keepdims=True)
        new_out = jnp.dot(expo.astype(BF16), both, preferred_element_type=F32)
        new_grad = jnp.dot(weighted.astype(BF16), key, preferred_element_type=F32)
        if first:
            row_sum[span, :] = total
            row_dot[span, :] = dot_total
            out_acc[span, :] = new_out
            grad_acc[span, :] = new_grad
        else:
            decay = jnp.exp(row_max[span, :] - top)
            row_sum[span, :] = decay * row_sum[span, :] + total
            row_dot[span, :] = decay * row_dot[span, :] + dot_total
            out_acc[span, :] = decay * out_acc[span, :] + new_out
            grad_acc[span, :] = decay * grad_acc[span, :] + new_grad
        row_max[span, :] = top

    diag = kv_ref[me]
    key_ids = diag[rows : rows + 1, :128].astype(F32)
    qi = lax.broadcasted_iota(jnp.int32, (rows, rows), 0)
    ki = lax.broadcasted_iota(jnp.int32, (rows, rows), 1)
    allowed = (my_ids == key_ids) & (ki <= qi)
    for head in range(2):
        part(head, diag[:rows], allowed, True)

    lane = lax.broadcasted_iota(jnp.int32, (1, 2 * rows), 1)

    def step(t, carry):
        upper = me - 2 * t
        start = jnp.maximum(upper - 2, 0)
        pair = [kv_ref[start], kv_ref[start + 1]]
        both = jnp.concatenate([p[:rows] for p in pair], axis=0)
        key_ids = jnp.concatenate([p[rows : rows + 1, :128] for p in pair], axis=1).astype(F32)
        key_ids = jnp.where(lane < (upper - start) * rows, key_ids, -1.0)
        allowed = my_ids == key_ids
        for head in range(2):
            part(head, both, allowed, False)
        return carry

    lax.fori_loop(0, (me - first_ref[0] + 1) // 2, step, 0)

    cosine, sine = cos_ref[...], sin_ref[...]
    for head in range(8):
        at = head * rows
        span = slice(at, at + rows)
        inverse = 1.0 / row_sum[span, :]
        out_ref[:, head * 128 : (head + 1) * 128] = (out_acc[span, 128:] * inverse).astype(BF16)
        mean_dot = row_dot[span, :] * inverse
        grad = soft_scale * inverse * (grad_acc[span, :] - mean_dot * out_acc[span, :128])
        turned = pltpu.roll(grad * sine, 64, 1)
        lin[:, head * 128 : (head + 1) * 128] = (grad * cosine + turned).astype(BF16)
    up_ref[...] = ADAPTER_SCALE * jnp.dot(lr_ref[...], lin[...], preferred_element_type=F32)
    middle = (ADAPTER_SCALE * nt(qup_ref[...], lin[...])).astype(BF16)
    ga_ref[...] = jnp.dot(middle, xn_ref[...], preferred_element_type=F32)


def rope_tables(place, rows):
    positions = (place * rows + jnp.arange(rows, dtype=jnp.int32)).astype(F32)
    half = HEAD_SIZE // 2
    freqs = jnp.exp(jnp.arange(half, dtype=F32) * (-2.0 * math.log(ROPE_BASE) / HEAD_SIZE))
    angle = positions[:, None] * freqs[None, :]
    cosine, sine = jnp.cos(angle), jnp.sin(angle)
    def planes(table):
        return jnp.transpose(table.T.reshape(8, 8, rows), (1, 0, 2)).reshape(half, rows)

    wide_cos = jnp.concatenate([cosine, cosine], axis=-1)
    wide_sin = jnp.concatenate([-sine, sine], axis=-1)
    return planes(cosine), planes(sine), wide_cos, wide_sin


def on_device(
    layer_input, gain, codes, column_scale_quantized, block_second_scale,
    query_down_map, query_up_map, token_document, output_cotangent,
):
    rows, width = layer_input.shape
    place = lax.axis_index("ctx")
    cos_t, sin_t, cos_w, sin_w = rope_tables(place, rows)
    vm = pl.BlockSpec(memory_space=pltpu.VMEM)
    sm = pl.BlockSpec(memory_space=pltpu.SMEM)
    blocks = column_scale_quantized.shape[0]
    rank = query_up_map.shape[0]
    kv_width = 4 * HEAD_SIZE
    q, kv, xn, lr = pl.pallas_call(
        proj_kernel,
        out_shape=(
            jax.ShapeDtypeStruct((rows, query_up_map.shape[1]), BF16),
            jax.ShapeDtypeStruct((rows + ID_ROWS, kv_width), BF16),
            jax.ShapeDtypeStruct((rows, width), BF16),
            jax.ShapeDtypeStruct((rank, rows), BF16),
        ),
        in_specs=[vm] * 10,
        out_specs=(vm,) * 4,
        scratch_shapes=[
            pltpu.VMEM((24, blocks, 128), F32),
            pltpu.VMEM((8, blocks, 128), F32),
            pltpu.VMEM((rows, 1024), F32),
            pltpu.VMEM((8, 128, rows), F32),
            pltpu.VMEM((8, 64, rows), F32),
            pltpu.VMEM((8, 64, rows), BF16),
            pltpu.VMEM((8, 64, rows), BF16),
            pltpu.VMEM((8, 128, rows), BF16),
            pltpu.VMEM((8, 128, rows), BF16),
            pltpu.SemaphoreType.DMA((2,)),
            pltpu.SemaphoreType.DMA((2,)),
        ],
        compiler_params=pltpu.CompilerParams(
            collective_id=0, has_side_effects=True, vmem_limit_bytes=56 * 1024 * 1024
        ),
        name="project",
    )(
        layer_input, gain[None, :], codes, column_scale_quantized, block_second_scale[:, None],
        query_down_map.T, query_up_map, token_document[None, :], cos_t, sin_t,
    )
    all_kv = lax.all_gather(kv, "ctx", axis=0, tiled=False)
    all_ids = all_kv[:, rows, :rows].astype(F32)
    needed = (all_ids[:, -1] >= token_document[0].astype(F32)) & (
        jnp.arange(all_ids.shape[0]) <= place
    )
    first = jnp.argmax(needed).astype(jnp.int32)[None]
    heads_rows = 8 * rows
    attn, up, ga = pl.pallas_call(
        attn_kernel,
        out_shape=(
            jax.ShapeDtypeStruct(output_cotangent.shape, BF16),
            jax.ShapeDtypeStruct(query_up_map.shape, F32),
            jax.ShapeDtypeStruct((rank, width), F32),
        ),
        in_specs=[sm] + [vm] * 9,
        out_specs=(vm,) * 3,
        scratch_shapes=[
            pltpu.VMEM((heads_rows, 128), BF16),
            pltpu.VMEM((heads_rows, 128), BF16),
            pltpu.VMEM((heads_rows, 1), F32),
            pltpu.VMEM((heads_rows, 1), F32),
            pltpu.VMEM((heads_rows, 1), F32),
            pltpu.VMEM((heads_rows, 256), F32),
            pltpu.VMEM((heads_rows, 128), F32),
            pltpu.VMEM((rows, 1024), BF16),
        ],
        compiler_params=pltpu.CompilerParams(vmem_limit_bytes=56 * 1024 * 1024),
        name="attend",
    )(
        first, q, output_cotangent, all_kv, token_document.astype(F32)[:, None], xn, lr,
        query_up_map, cos_w, sin_w,
    )
    up = lax.psum(up, "ctx")
    ga = lax.psum(ga, ("ctx", "fsdp"))
    return attn, ga.T, up


def solution(mesh):
    return jax.shard_map(
        on_device,
        mesh=mesh,
        in_specs=(
            P("ctx", None),
            P(),
            P("fsdp", None),
            P("fsdp", None),
            P(),
            P(),
            P(None, "fsdp"),
            P("ctx"),
            P("ctx", "fsdp"),
        ),
        out_specs=(P("ctx", "fsdp"), P(), P(None, "fsdp")),
        check_vma=False,
    )
```

time: 609 us -> 335 us (0.55); the launches traced: 597 us -> 334 us
  local copies, waits for them, and re-layouts: 160 us -> 6.1 us
  matrix products: 51.8 us -> 0 us
  waiting for transfers between devices: 326 us -> 275 us
  Pallas kernels: 0 us -> 36 us
  blocking collectives: 34.1 us -> 0 us
  other arithmetic: 9.96 us -> 2.83 us
    another operation x9 -> x0, local copies, waits for them, and re-layouts: 112 us -> none  [dequantize(): jnp.stack(pieces, axis=-1).reshape(row_count, packed.shape[1] * 8)]
    dot_general x10 -> x0, matrix products: 51.8 us -> none  [the longest x1 42.3 us: on_device(): jnp.dot(input_normalized, weight, preferred_element_type=jnp.float32)]
    all_gather x3 -> x1, waiting for transfers between devices: 85.2 us -> 41.1 us  [on_device(): all_kv = lax.all_gather(kv, 'ctx', axis=0, tiled=False)]
    mul x2 -> x0, local copies, waits for them, and re-layouts: 36.7 us -> none  [dequantize(): scaled = levels.reshape(row_count // 64, 64, -1) * absmax[:, None, :]]
    pallas_call x0 -> x2, Pallas kernels: none -> 36 us  [the longest x1 30.5 us: on_device(): pl.pallas_call(proj_kernel, out_shape=(jax.ShapeDtypeStruct((rows, query_...]
    all_gather x2 -> x0, blocking collectives: 34.1 us -> none  [the longest x1 21.3 us: on_device(): all_ids = lax.all_gather(token_document, 'ctx', axis=0, tiled=True)]
    psum x2, waiting for transfers between devices: 241 us -> 234 us  [the longest x1 134 us: on_device(): ga = lax.psum(ga, ('ctx', 'fsdp'))]
    and x2 -> x0, other arithmetic: 6.37 us -> none  [the longest x1 6.17 us: dequantize(): jnp.bitwise_and(jnp.right_shift(packed, 4 * nibble), 15)]
  transfers between devices with their start and end apart: 5 -> 3, of which waited for: 5 -> 3; matrix products, arithmetic and copies ran while one was open for 7% -> 1% of each run, Pallas kernels for 0% -> 0%
where the time goes in v1:
time: 335 us; the launch traced here: 334 us
  waiting for transfers between devices  275 us (82%)
  Pallas kernels  36 us (11%)
  between operations  13.8 us (4%)
  local copies, waits for them, and re-layouts  6.1 us (2%)
    psum x1, waiting for transfers between devices, on_device(): ga = lax.psum(ga, ('ctx', 'fsdp'))  134 us
    psum x1, waiting for transfers between devices, on_device(): up = lax.psum(up, 'ctx')  99.3 us
    all_gather x1, waiting for transfers between devices, on_device(): all_kv = lax.all_gather(kv, 'ctx', axis=0, tiled=False)  41.1 us
    pallas_call x1, Pallas kernels, on_device(): pl.pallas_call(proj_kernel, out_shape=(jax.ShapeDtypeStruct((rows, query_...  30.5 us
  transfers between devices with their start and end apart: 3, of which 3 were waited for; matrix products, arithmetic and copies ran while one was open for 1% of the time, Pallas kernels for 0%

profile of v1, /device:TPU:0, one launch (start us, length us, event | category | flops | bytes accessed | tf_op | source)
XLA Modules:
  0.0 334.3 jit_solution(16420975947894687694)
XLA Ops:
  7.2 0.0 copy-start
  7.2 0.0 all-gather.3.cloned.1.call-start
  7.3 0.1 exp.16
  7.3 1.4 copy.14.bss_ref
  8.7 0.8 multiply_sine_fusion.1
  9.5 30.5 %project.1 = (bf16[128,1024]{1,0:T(8,128)(2,1)}, bf16[144,512]{1,0:T(8,128)(2,1)}, bf16[128,4096]{1,0:T(8,128)(2,1)}, bf16[16,128]{1,0:T(8,128)(2,1)}) custom-call(bf16[128,4096]{1,0:T(8,128)(2,1)} %x_ref.1, f32[1,4096]{1,0:T(1,128)} %bitcast.18, s32[2048,384]{1,0:T(8,128)} %codes_ref.1, s32[32,3072]{1,0:T(8,128)} %cs_ref.1, f32[64,1]{1,0:T(8,128)} %copy.14.bss_ref, ...), custom_call_target="tpu_custom_call" | custom-call | tf_op jit(solution)/shard_map/project/pallas_call | solution.py:317
  40.0 0.0 all-gather.3.cloned.1.call-update
  40.1 0.0 all-reduce.5.cloned.1.call-start
  40.1 0.0 copy-done
  40.2 0.7 copy.15.ids_ref
  40.9 0.3 fusion
  41.2 0.8 pad_maximum_fusion
  42.0 41.1 %all-gather.3.cloned.1.call-done = bf16[2304,512]{1,0:T(8,128)(2,1)} async-done(((bf16[144,512]{1,0:T(8,128)(2,1)}), bf16[2304,512]{1,0:T(8,128)(2,1)}) %all-gather.3.cloned.1.call-update) | async-done | bytes 2359312 | tf_op jit(solution)/shard_map/all_gather | solution.py:348
  83.0 0.8 slice.16
  83.8 0.2 fusion.1
  84.0 0.7 and_reduce_fusion
  84.7 5.5 %attend.1 = (bf16[128,1024]{1,0:T(8,128)(2,1)}, f32[16,1024]{1,0:T(8,128)}, f32[16,4096]{1,0:T(8,128)}) custom-call(s32[1]{0:T(128)} %bitcast.6.first_ref, bf16[128,1024]{1,0:T(8,128)(2,1)} %get-tuple-element.13.q_ref, bf16[128,1024]{1,0:T(8,128)(2,1)} %do_ref.1, bf16[16,144,512]{2,1,0:T(8,128)(2,1)} %bitcast.15, f32[128,1]{1,0:T(8,128)} %copy.15.ids_ref, ...), custom_call_target="tpu_custom_call" | custom-call | tf_op jit(solution)/shard_map/attend/pallas_call | solution.py:355
  90.3 0.0 all-reduce.5.cloned.1.call-update
  90.3 0.0 all-reduce.3.cloned.1.call-start
  90.3 0.7 all-reduce.3.cloned.1.call-update
  91.0 99.3 %all-reduce.5.cloned.1.call-done = f32[16,1024]{1,0:T(8,128)} async-done(((f32[16,1024]{1,0:T(8,128)}), f32[16,1024]{1,0:T(8,128)}) %all-reduce.5.cloned.1.call-update) | async-done | bytes 65552 | tf_op jit(solution)/shard_map/psum | solution.py:380
  190.4 134.2 %all-reduce.3.cloned.1.call-done = f32[4096,16]{0,1:T(8,128)} async-done(((f32[4096,16]{0,1:T(8,128)}), f32[4096,16]{0,1:T(8,128)}) %all-reduce.3.cloned.1.call-update) | async-done | bytes 262160 | tf_op jit(solution)/shard_map/psum | solution.py:381
  324.6 1.7 copy.21
  326.3 1.5 copy.22
  (5 shorter events, 0.0 us)
Async XLA Ops:
  7.2 32.9 %copy-start = (s32[128]{0:T(128)S(1)}, s32[128]{0:T(128)}, u32[]{:S(2)}) copy-start(s32[128]{0:T(128)} %param.16) | copy-start | bytes 1540
  7.2 75.9 %all-gather.3.cloned.1.call-start = ((), (), s32[]{:S(2)}) async-start(), calls=%async_computation.2 | async-start | bytes 2506752 | tf_op jit(solution)/shard_map/all_gather | solution.py:348
  40.1 150.3 %all-reduce.5.cloned.1.call-start = ((), (), s32[]{:S(2)}) async-start(), calls=%async_computation.1 | async-start | bytes 131072 | tf_op jit(solution)/shard_map/psum | solution.py:380
  90.3 234.3 %all-reduce.3.cloned.1.call-start = ((), (), s32[]{:S(2)}) async-start(), calls=%async_computation | async-start | bytes 524288 | tf_op jit(solution)/shard_map/psum | solution.py:381
Sparse Core Ops, SparseCore 0:
  40.2 42.8 all-gather.2
  90.4 99.9 all-reduce.4
  196.4 128.1 all-reduce.2
